TPU v7x, 256 devices: a whole 4x4x8 slice. The times are simulated.
256 devices in a mesh: seq: 64 (over z, y, core), head: 4 (over x).
Axes of the slice: x: 4, y: 4, z: 8, core: 2. Of those that a mesh axis runs over, the one named last changes fastest.
Arguments:
- query_rows: bfloat16 [32768, 4096], P('seq', 'head'), may hold values from -6 to 6
- key_rows: bfloat16 [32768, 4096], P('seq', 'head'), may hold values from -2 to 2
- value_rows: bfloat16 [32768, 4096], P('seq', 'head'), may hold values from -6 to 6
- key_gain: float32 [32], P('head'), may hold values from 0.9 to 1.85, as said below
- regularizer: float32 [32], P('head'), may hold values from 0.5 to 4
Outputs:
- readout: bfloat16 [32768, 4096], P('seq', 'head')
Inputs may be any that keep to these rules, and one draw needn't show every extreme that they name: `key_gain`: one positive gain for each head.
All inputs are finite; a program needn't handle non-finite values.
Results may differ from a plain program's by a relative error of at most 0.006.
Values sent between devices are 32-bit elements; how exact they have to be, the bound alone decides.
A program may use at most 192 MiB of HBM per device.

v0:
```python
import jax
import jax.numpy as jnp
from jax import lax
from jax.sharding import Mesh
from jax.sharding import PartitionSpec as P

DH = 128
NS_STEPS = 8
REFINE = 2
SEQ = ("seq_0", "seq_1", "seq_2")


highest = lax.Precision.HIGHEST


def filled_with(value, identity):
    return jnp.zeros_like(value) + jnp.asarray(identity, value.dtype)


def prefix_by_axis(value, axes, combine, identity):
    before = start = filled_with(value, identity)
    subtotal = value
    for axis in reversed(axes):
        length, place = (lax.axis_size(axis), lax.axis_index(axis))
        pieces = lax.all_gather(subtotal, axis)
        inside, subtotal = (start, start)
        for k in range(length):
            passed = k < place
            subtotal = combine(subtotal, pieces[k])
            inside = jnp.where(passed, subtotal, inside)
        before = combine(inside, before)
    return before


def contract_rows(left, right):
    return lax.dot_general(
        left, right, (((1,), (1,)), ((), ())), preferred_element_type=jnp.float32
    )


def add_states(earlier, later):
    return earlier + later


def invert_scaled(end_matrix, spectral_bound):
    identity = jnp.eye(end_matrix.shape[-1], dtype=jnp.float32)
    approx = identity[None, :, :] / spectral_bound[:, None, None]
    for iteration in range(NS_STEPS):
        product = jnp.einsum("hij,hjk->hik", end_matrix, approx, precision=highest)
        approx = jnp.einsum("hij,hjk->hik", approx, 2.0 * identity - product, precision=highest)
    return approx


def solve_head(operands):
    query_head, key_head, value_head, base_matrix, precond, cross_matrix = operands
    length = query_head.shape[0]
    causal = jnp.arange(length)[:, None] >= jnp.arange(length)[None, :]
    query_float = query_head.astype(jnp.float32)
    solution = jnp.dot(query_float, precond, precision=highest)
    for repeat in range(REFINE):
        scores = jnp.where(
            causal, contract_rows(solution.astype(jnp.bfloat16), key_head), 0.0
        ).astype(jnp.bfloat16)
        in_block = jnp.dot(scores, key_head, preferred_element_type=jnp.float32)
        residual = query_float - jnp.dot(solution, base_matrix, precision=highest) - in_block
        solution = solution + jnp.dot(residual, precond, precision=highest)
    scores = jnp.where(causal, contract_rows(solution.astype(jnp.bfloat16), key_head), 0.0).astype(
        jnp.bfloat16
    )
    total = jnp.dot(solution, cross_matrix, precision=highest) + jnp.dot(
        scores, value_head, preferred_element_type=jnp.float32
    )
    return total.astype(jnp.bfloat16)


def body(query_rows, key_rows, value_rows, key_gain, regularizer):
    row_count = query_rows.shape[0]
    head_count = key_gain.shape[0]
    query_split = query_rows.reshape(row_count, head_count, DH)
    key_split = key_rows.reshape(row_count, head_count, DH)
    value_split = value_rows.reshape(row_count, head_count, DH)
    scaled = (key_split.astype(jnp.float32) * key_gain[None, :, None]).astype(jnp.bfloat16)
    gram_block = jnp.einsum("thd,the->hde", scaled, scaled, preferred_element_type=jnp.float32)
    cross_block = jnp.einsum(
        "thd,the->hde", scaled, value_split, preferred_element_type=jnp.float32
    )
    payload = jnp.stack([gram_block, cross_block])
    earlier = prefix_by_axis(payload, SEQ, add_states, jnp.zeros_like(payload))
    earlier_gram = earlier[0]
    earlier_cross = earlier[1]
    identity = jnp.eye(DH, dtype=jnp.float32)
    base_matrix = regularizer[:, None, None] * identity + earlier_gram
    end_matrix = base_matrix + gram_block
    spectral_bound = jnp.sqrt(jnp.sum(end_matrix * end_matrix, axis=(1, 2)))
    precond = invert_scaled(end_matrix, spectral_bound)
    readout = lax.map(
        solve_head,
        (
            jnp.transpose(query_split, (1, 0, 2)),
            jnp.transpose(scaled, (1, 0, 2)),
            jnp.transpose(value_split, (1, 0, 2)),
            base_matrix,
            precond,
            earlier_cross,
        ),
    )
    return jnp.transpose(readout, (1, 0, 2)).reshape(row_count, head_count * DH)


def solution(mesh):
    torus = Mesh(
        mesh.devices.reshape(8, 4, 2, mesh.shape["head"]), ("seq_0", "seq_1", "seq_2", "head")
    )
    in_specs = (P(SEQ, "head"), P(SEQ, "head"), P(SEQ, "head"), P("head"), P("head"))
    out_specs = P(SEQ, "head")
    return jax.shard_map(body, mesh=torus, in_specs=in_specs, out_specs=out_specs, check_vma=False)
```

profile of v0, /device:TPU:1, one launch (start us, length us, event | category | flops | bytes accessed | tf_op | source)
XLA Modules:
  0.0 289.9 jit_solution(16953520821809289704)
XLA Ops:
  6.5 1.6 copy.19
  11.2 20.5 %all-gather.8.cloned.1.call-done = f32[4,8,128,128]{3,2,1,0:T(8,128)} async-done(((f32[2,8,128,128]{3,2,1,0:T(8,128)}), f32[4,8,128,128]{3,2,1,0:T(8,128)}) %all-gather.8.cloned.1.call-update) | async-done | bytes 2097168 | tf_op jit(solution)/shard_map/all_gather | solution.py:25
  31.8 2.6 slice_add_fusion.10
  34.5 51.3 %all-gather.10.cloned.1.call-done = f32[8,8,128,128]{3,2,1,0:T(8,128)} async-done(((f32[2,8,128,128]{3,2,1,0:T(8,128)}), f32[8,8,128,128]{3,2,1,0:T(8,128)}) %all-gather.10.cloned.1.call-update) | async-done | bytes 4194320 | tf_op jit(solution)/shard_map/all_gather | solution.py:25
  85.8 3.5 %fusion.68 = f32[1,2,8,128,128]{4,3,2,1,0:T(8,128)} fusion(f32[8,8,128,128]{3,2,1,0:T(8,128)} %all-gather.10.cloned.1.call-done), kind=kLoop, calls=%fused_computation.84 | loop fusion | flops 786432 | bytes 5242880 | tf_op jit(solution)/shard_map/add | solution.py:42
  89.3 2.4 copy.18
  93.1 90.7 %all-gather.6.cloned.1.call-done = f32[8,2,8,128,128]{4,3,2,1,0:T(8,128)} async-done(((f32[1,2,8,128,128]{4,3,2,1,0:T(8,128)}), f32[8,2,8,128,128]{4,3,2,1,0:T(8,128)}) %all-gather.6.cloned.1.call-update) | async-done | bytes 8388624 | tf_op jit(solution)/shard_map/all_gather | solution.py:25
  183.8 6.4 %fusion.67 = f32[1,2,8,128,128]{4,3,2,1,0:T(8,128)S(1)} fusion(f32[8,2,8,128,128]{4,3,2,1,0:T(8,128)} %all-gather.6.cloned.1.call-done, f32[8,8,128,128]{3,2,1,0:T(8,128)} %all-gather.10.cloned.1.call-done, f32[4,8,128,128]{3,2,1,0:T(8,128)S(1)} %copy-done, pred[]{:T(512)S(6)} %gt.51, pred[]{:T(512)S(6)} %gt.52, pred[]{:T(512)S(6)} %gt.53, pred[]{:T(512)S(6)} %gt.54, ...), kind=kLoop, calls=%fused_computation.76 | loop fusion | flops 7077888 | bytes 15728654 | tf_op jit(solution)/shard_map/add | solution.py:42
  202.1 78.9 %while.10 = (s32[]{:T(128)}, bf16[8,512,128]{2,1,0:T(8,128)(2,1)}, bf16[8,512,128]{1,2,0:T(8,128)(2,1)}, f32[8,128,128]{2,1,0:T(8,128)S(1)}, f32[8,128,128]{2,1,...) while((s32[]{:T(128)}, bf16[8,512,128]{2,1,0:T(8,128)(2,1)}, ...), condition=%wide.region_2.3_spmd, body=%wide.region_1.2_spmd.sunk | while | flops 1009844224 | bytes 7738481 | solution.py:96
  204.8 1.4 fusion.176
  207.0 1.4 fusion.177
  210.0 2.1 fusion.179
  214.7 1.4 fusion.176
  216.8 1.4 fusion.177
  219.8 2.0 fusion.179
  224.5 1.4 fusion.176
  226.7 1.4 fusion.177
  229.7 2.0 fusion.179
  234.4 1.4 fusion.176
  236.5 1.4 fusion.177
  239.5 2.0 fusion.179
  244.2 1.4 fusion.176
  246.4 1.4 fusion.177
  249.4 2.0 fusion.179
  254.1 1.4 fusion.176
  259.3 2.1 fusion.179
  266.1 1.4 fusion.177
  269.1 2.0 fusion.179
  273.8 1.4 fusion.176
  276.0 1.4 fusion.177
  279.0 2.0 fusion.179
  281.0 2.4 copy_bitcast_fusion
  (113 shorter events, 58.6 us)
Async XLA Ops:
  6.5 1.6 copy-start.4
  6.5 2.2 copy-start.5
  6.5 25.2 %all-gather.8.cloned.1.call-start = ((), (), s32[]{:S(2)}) async-start(), calls=%async_computation.1 | async-start | bytes 3145728 | tf_op jit(solution)/shard_map/all_gather | solution.py:25
  8.7 1.1 copy-start.1
  9.3 0.8 copy-start.2
  11.2 74.6 %all-gather.10.cloned.1.call-start = ((), (), s32[]{:S(2)}) async-start(), calls=%async_computation.2 | async-start | bytes 5242880 | tf_op jit(solution)/shard_map/all_gather | solution.py:25
  34.4 149.4 %all-gather.6.cloned.1.call-start = ((), (), s32[]{:S(2)}) async-start(), calls=%async_computation | async-start | bytes 9437184 | tf_op jit(solution)/shard_map/all_gather | solution.py:25
  89.3 94.5 %copy-start = (f32[4,8,128,128]{3,2,1,0:T(8,128)S(1)}, f32[4,8,128,128]{3,2,1,0:T(8,128)}, u32[]{:S(2)}) copy-start(f32[4,8,128,128]{3,2,1,0:T(8,128)} %all-gather.8.cloned.1.call-done) | copy-start | bytes 6291460
  93.1 97.9 %copy-start.3 = (f32[8,128,128]{2,1,0:T(8,128)S(1)}, f32[8,128,128]{2,1,0:T(8,128)}, u32[]{:S(2)}) copy-start(f32[8,128,128]{2,1,0:T(8,128)} %copy-done.2) | copy-start | bytes 1572868
  93.1 97.9 %copy-start.6 = (f32[8]{0:T(128)S(1)}, f32[8]{0:T(128)}, u32[]{:S(2)}) copy-start(f32[8]{0:T(128)} %param.11) | copy-start | bytes 100
Sparse Core Ops, SparseCore 0:
  11.3 20.4 all-gather.7
  34.5 51.1 all-gather.9
  89.4 94.4 all-gather.5
where the time goes:
time: 291 us; the launch traced here: 290 us
  waiting for transfers between devices  163 us (56%)
  matrix products  81.8 us (28%)
  local copies, waits for them, and re-layouts  16.4 us (6%)
  other arithmetic  15.2 us (5%)
  between operations  13.4 us (5%)
    all_gather x3, waiting for transfers between devices, prefix_by_axis(): pieces = lax.all_gather(subtotal, axis)  163 us
    dot_general x16, matrix products, solve_head(): in_block = jnp.dot(scores, key_head, preferred_element_type=jnp.float32)  22.5 us
    dot_general x8, matrix products, solve_head(): jnp.dot(scores, value_head, preferred_element_type=jnp.float32)  16.4 us
    add x3, other arithmetic, add_states(): return earlier + later  12.5 us
    dot_general x8, matrix products, solve_head(): solution = jnp.dot(query_float, precond, precision=highest)  9.74 us
    dot_general x8, matrix products, solve_head(): jnp.dot(solution, cross_matrix, precision=highest)  9.65 us
    dynamic_slice x16, local copies, waits for them, and re-layouts, body(): lax.map(solve_head, (jnp.transpose(query_split, (1, 0, 2)), jnp.transpose...  8.29 us
    dot_general x16, matrix products, solve_head(): jnp.dot(solution, base_matrix, precision=highest)  5.95 us
  transfers between devices with their start and end apart: 3, of which 3 were waited for; matrix products, arithmetic and copies ran while one was open for 1% of the time, Pallas kernels for 0%

commit v1 on v0

v1 whole, which is shorter than its diff:
```python
import functools

import jax
import jax.numpy as jnp
from jax import lax
from jax.experimental import pallas as pl
from jax.experimental.pallas import tpu as pltpu
from jax.sharding import Mesh
from jax.sharding import PartitionSpec as P

DH = 128
NS_STEPS = 8
REFINE = 2
SEQ = ("seq_0", "seq_1", "seq_2")
MESH = pl.DeviceIdType.MESH
F32, BF16 = jnp.float32, jnp.bfloat16


def dot(a, b):
    return jnp.dot(a, b, preferred_element_type=F32)


def dot_general(a, b, left, right):
    return lax.dot_general(a, b, (((left,), (right,)), ((), ())), preferred_element_type=F32)


def split(x):
    high = x.astype(BF16)
    low = (x - high.astype(F32)).astype(BF16)
    return high, low


def side(x):
    return jnp.concatenate(split(x), axis=1)


def square(x):
    row = side(x)
    return jnp.concatenate([row, row], axis=0)


def fold(p):
    return p[:, :DH] + p[:, DH:]


def iota(shape, dim):
    return lax.broadcasted_iota(jnp.int32, shape, dim)


def pack_gram(gram):
    half = DH // 2
    top, bottom = gram[:half], gram[half:]
    r, c = iota((half, DH), 0), iota((half, DH), 1)
    rolled = pltpu.roll(bottom, half, 1)
    packed = jnp.where((c < half) & (r < c), rolled, top)
    diagonal = jnp.sum(jnp.where(c == r + half, bottom, 0.0), axis=0, keepdims=True)
    return packed, diagonal


def unpack_gram(packed, diagonal):
    half = DH // 2
    r, c = iota((half, DH), 0), iota((half, DH), 1)
    flipped = jnp.concatenate([packed, packed], axis=0).T
    upper_flip, lower_flip = flipped[:half], flipped[half:]
    top = jnp.where((c < half) & (r < c), upper_flip, packed)
    a22 = pltpu.roll(jnp.where(r < c, packed, upper_flip), half, 1)
    bottom = jnp.where(c < half, lower_flip, jnp.where(c == r + half, diagonal, a22))
    return jnp.concatenate([top, bottom], axis=0)


def kernel(
    dims, gain, ridge, q_hbm, k_hbm, v_hbm, o_hbm,
    q, k, v, o, ks, shi, slo, own, state, bcat, ycat, ccat,
    gp, gin, gt, gf, gs, gr, xp, xin, xt, xf, xs, xr,
    load_sem, out_sem, pair_send, pair_recv, send_sem, recv_sem,
):
    nz, ny, heads, tokens = dims
    chips = nz * ny
    pieces = 8 * heads
    mine = pieces // 2
    per = mine // chips
    z, y, core = (lax.axis_index(a) for a in SEQ)
    chip = z * ny + y
    base_piece = core * mine

    def where_is(j):
        return {"seq_0": j // ny, "seq_1": j % ny}

    loads = []
    for n, (src, dst) in enumerate(((k_hbm, k), (v_hbm, v), (q_hbm, q))):
        copy = pltpu.make_async_copy(src, dst, load_sem.at[n])
        copy.start()
        loads.append(copy)

    barrier = pltpu.get_barrier_semaphore()
    pl.semaphore_signal(barrier, inc=1, device_id={"seq_2": 1 - core}, device_id_type=MESH)

    @pl.loop(1, chips)
    def _(d):
        pl.semaphore_signal(
            barrier, inc=1, device_id=where_is((chip + d) % chips), device_id_type=MESH
        )

    loads[0].wait()
    loads[1].wait()
    for h in range(heads):
        cols = slice(h * DH, (h + 1) * DH)
        scaled = (k[:, cols].astype(F32) * gain[h]).astype(BF16)
        ks[:, cols] = scaled
        both = dot_general(scaled, jnp.concatenate([scaled, v[:, cols]], axis=1), 0, 0)
        gram, cross = both[:, :DH], both[:, DH:]
        own[h] = gram
        packed, diagonal = pack_gram(gram)
        rows = slice(h * 8, (h + 1) * 8)
        gp[rows, 0:8, :] = packed.reshape(8, 8, DH)
        gp[rows, 8:9, :] = jnp.broadcast_to(diagonal.reshape(1, 1, DH), (8, 1, DH))
        xp[rows] = cross.reshape(8, 16, DH)
    pl.semaphore_wait(barrier, chips)

    def to_partner(src, dst, n):
        return pltpu.make_async_remote_copy(
            src_ref=src, dst_ref=dst, send_sem=pair_send.at[n], recv_sem=pair_recv.at[n],
            device_id={"seq_2": 1 - core}, device_id_type=MESH,
        )

    def to_chip(src, dst, group, there, slot):
        return pltpu.make_async_remote_copy(
            src_ref=src, dst_ref=dst, send_sem=send_sem.at[group, there],
            recv_sem=recv_sem.at[group, slot], device_id=where_is(there), device_id_type=MESH,
        )

    def slot(ref, j):
        return ref.at[pl.ds(j * per, per)]

    def half_slot(ref, j):
        return ref.at[pl.ds(base_piece + j * per, per)]

    def outward(part, came, total, found, group):
        total[...] = part[pl.ds(base_piece, mine)] + came[pl.ds(base_piece, mine)]
        found[pl.ds(chip * per, per)] = total[pl.ds(chip * per, per)]

        @pl.loop(1, chips)
        def _(d):
            there = (chip + d) % chips
            to_chip(slot(total, there), slot(found, chip), group, there, chip).start()

    def homeward(total, found, sums, result, group):
        def body(j, running):
            @pl.when(j != chip)
            def _():
                to_chip(slot(total, j), slot(found, j), group, j, j).wait_recv()

            sums[pl.ds(j * per, per)] = running

            @pl.when(j != chip)
            def _():
                to_chip(slot(sums, j), half_slot(result, chip), group + 1, j, chip).start()

            @pl.when(j == chip)
            def _():
                result[pl.ds(base_piece + chip * per, per)] = running

            return running + found[pl.ds(j * per, per)]

        lax.fori_loop(0, chips, body, jnp.zeros((per,) + found.shape[1:], F32))

    def gather(sums, result, group):
        @pl.loop(1, chips)
        def _(d):
            there = (chip + d) % chips
            to_chip(slot(sums, there), half_slot(result, there), group + 1, there, there).wait_recv()

    def drain(total, sums, found, result, group):
        @pl.loop(1, chips)
        def _(d):
            there = (chip + d) % chips
            to_chip(slot(total, there), slot(found, chip), group, there, chip).wait_send()
            to_chip(slot(sums, there), half_slot(result, chip), group + 1, there, chip).wait_send()

    def my_half(ref):
        return ref.at[pl.ds(base_piece, mine)]

    gram_pair = to_partner(gp, gin, 0)
    gram_pair.start()
    cross_pair = to_partner(xp, xin, 1)
    cross_pair.start()
    gram_pair.wait_recv()
    outward(gp, gin, gt, gf, 0)
    homeward(gt, gf, gs, gr, 0)
    cross_pair.wait_recv()
    outward(xp, xin, xt, xf, 2)
    gather(gs, gr, 0)
    gram_back = to_partner(my_half(gr), my_half(gr), 2)
    gram_back.start()
    gram_back.wait_recv()

    second = core == 1
    eye = jnp.where(iota((DH, DH), 0) == iota((DH, DH), 1), 1.0, 0.0)
    for h in range(heads):
        rows = slice(h * 8, (h + 1) * 8)
        whole = gr[rows] + jnp.where(second, gin[rows], 0.0)
        prior = unpack_gram(whole[:, 0:8, :].reshape(DH // 2, DH), whole[0, 8:9, :])
        base = prior + ridge[h] * eye
        bcat[h] = square(base)
        end = base + own[h]
        total = jnp.sum(jnp.sum(end * end, axis=1, keepdims=True), axis=0, keepdims=True)
        inverse = 1.0 / jnp.sqrt(total)
        state[h, :DH] = eye
        state[h, DH:] = end * inverse
        own[h] = jnp.broadcast_to(inverse, (DH, DH))

    @pl.loop(0, NS_STEPS)
    def _(step):
        for h in range(heads):
            x = state[h]
            left = side(x)
            row = left[DH:]
            product = dot(left, jnp.concatenate([row, row], axis=0))
            state[h] = 2.0 * x - fold(product)

    for h in range(heads):
        ycat[h] = square(state[h, :DH] * own[h])

    homeward(xt, xf, xs, xr, 2)
    loads[2].wait()

    block = 256
    causal = iota((block, block), 0) >= iota((block, block), 1)

    def scores_of(high, keys, count):
        s = dot_general(high, keys, 1, 1)
        if count == 1:
            return jnp.where(causal, s, 0.0).astype(BF16)
        past = s[:, : (count - 1) * block].astype(BF16)
        return jnp.concatenate(
            [past, jnp.where(causal, s[:, (count - 1) * block :], 0.0).astype(BF16)], axis=1
        )

    def columns(h):
        return pl.ds(pl.multiple_of(h * DH, DH), DH)

    @pl.loop(0, heads // 2)
    def _(pair):
        for which in range(2):
            h = pair * 2 + which
            cols = columns(h)
            for r in range(tokens // block):
                rows = slice(r * block, (r + 1) * block)
                query = q[rows, cols]
                keys = ks[0 : (r + 1) * block, cols]
                solution = fold(dot(query, ycat[h, :DH]))
                for repeat in range(REFINE):
                    high, low = split(solution)
                    in_block = dot(scores_of(high, keys, r + 1), keys)
                    through = fold(dot(jnp.concatenate([high, low], axis=1), bcat[h]))
                    residual = query.astype(F32) - through - in_block
                    solution = solution + fold(dot(side(residual), ycat[h]))
                high, low = split(solution)
                shi[rows, cols] = high
                slo[rows, cols] = low

    gather(xs, xr, 2)
    cross_back = to_partner(my_half(xr), my_half(xr), 3)
    cross_back.start()
    cross_back.wait_recv()
    for h in range(heads):
        rows = slice(h * 8, (h + 1) * 8)
        ccat[h] = square((xr[rows] + jnp.where(second, xin[rows], 0.0)).reshape(DH, DH))

    @pl.loop(0, heads // 2)
    def _(pair):
        for which in range(2):
            h = pair * 2 + which
            cols = columns(h)
            for r in range(tokens // block):
                rows = slice(r * block, (r + 1) * block)
                high, low = shi[rows, cols], slo[rows, cols]
                seen = slice(0, (r + 1) * block)
                scores = scores_of(high, ks[seen, cols], r + 1)
                total = fold(dot(jnp.concatenate([high, low], axis=1), ccat[h])) + dot(
                    scores, v[seen, cols]
                )
                o[rows, cols] = total.astype(BF16)
        both = pl.ds(pl.multiple_of(pair * 2 * DH, 2 * DH), 2 * DH)
        pltpu.make_async_copy(o.at[:, both], o_hbm.at[:, both], out_sem.at[pair]).start()

    @pl.loop(0, heads // 2)
    def _(pair):
        both = pl.ds(pl.multiple_of(pair * 2 * DH, 2 * DH), 2 * DH)
        pltpu.make_async_copy(o.at[:, both], o_hbm.at[:, both], out_sem.at[pair]).wait()

    drain(gt, gs, gf, gr, 0)
    drain(xt, xs, xf, xr, 2)
    for copy in (gram_pair, cross_pair, gram_back, cross_back):
        copy.wait_send()


def body(dims, query_rows, key_rows, value_rows, key_gain, regularizer):
    tokens, width = query_rows.shape
    heads = key_gain.shape[0]
    nz, ny = dims
    chips = nz * ny
    pieces = 8 * heads
    mine = pieces // 2
    rows = pltpu.VMEM((tokens, width), BF16)

    def exchange(depth):
        whole = pltpu.VMEM((pieces, depth, DH), F32)
        half = pltpu.VMEM((mine, depth, DH), F32)
        return [whole, whole, half, half, half, whole]

    cat = pltpu.VMEM((heads, 2 * DH, 2 * DH), BF16)
    return pl.pallas_call(
        functools.partial(kernel, (nz, ny, heads, tokens)),
        out_shape=jax.ShapeDtypeStruct((tokens, width), BF16),
        in_specs=[pl.BlockSpec(memory_space=pltpu.SMEM)] * 2
        + [pl.BlockSpec(memory_space=pl.ANY)] * 3,
        out_specs=pl.BlockSpec(memory_space=pl.ANY),
        scratch_shapes=[rows] * 7
        + [pltpu.VMEM((heads, DH, DH), F32), pltpu.VMEM((heads, 2 * DH, DH), F32), cat, cat, cat]
        + exchange(9)
        + exchange(16)
        + [
            pltpu.SemaphoreType.DMA((3,)),
            pltpu.SemaphoreType.DMA((heads // 2,)),
            pltpu.SemaphoreType.DMA((4,)),
            pltpu.SemaphoreType.DMA((4,)),
            pltpu.SemaphoreType.DMA((4, chips)),
            pltpu.SemaphoreType.DMA((4, chips)),
        ],
        compiler_params=pltpu.CompilerParams(collective_id=0, has_side_effects=True),
    )(key_gain, regularizer, query_rows, key_rows, value_rows)


def solution(mesh):
    nz, ny, cores = 8, 4, 2
    torus = Mesh(
        mesh.devices.reshape(nz, ny, cores, mesh.shape["head"]), SEQ + ("head",)
    )
    in_specs = (P(SEQ, "head"), P(SEQ, "head"), P(SEQ, "head"), P("head"), P("head"))
    return jax.shard_map(
        functools.partial(body, (nz, ny)), mesh=torus, in_specs=in_specs,
        out_specs=P(SEQ, "head"), check_vma=False,
    )
```

time: 291 us -> 59.6 us (0.20)
  waiting for transfers between devices: 163 us -> 0 us
  matrix products: 81.8 us -> 0 us
  Pallas kernels: 0 us -> 57.2 us
  other arithmetic: 15.2 us -> 0 us
  local copies, waits for them, and re-layouts: 16.4 us -> 2.26 us
  between operations: 13.4 us -> 0.01 us
    all_gather x3 -> x0, waiting for transfers between devices: 163 us -> none  [prefix_by_axis(): pieces = lax.all_gather(subtotal, axis)]
    dot_general x90 -> x0, matrix products: 81.8 us -> none  [the longest x16 22.5 us: solve_head(): in_block = jnp.dot(scores, key_head, preferred_element_type=jnp.float32)]
    pallas_call x0 -> x1, Pallas kernels: none -> 57.2 us  [body(): pl.pallas_call(functools.partial(kernel, (nz, ny, heads, tokens)), out_sh...]
    add x3 -> x0, other arithmetic: 12.5 us -> none  [add_states(): return earlier + later]
    dynamic_slice x16 -> x0, local copies, waits for them, and re-layouts: 8.29 us -> none  [body(): lax.map(solve_head, (jnp.transpose(query_split, (1, 0, 2)), jnp.transpose...]
  transfers between devices with their start and end apart: 3 -> 0, of which waited for: 3 -> 0; matrix products, arithmetic and copies ran while one was open for 1% -> 0% of each run, Pallas kernels for 0% -> 0%
where the time goes in v1:
time: 59.6 us; the launch traced here: 59.4 us
  Pallas kernels  57.2 us (96%)
  local copies, waits for them, and re-layouts  2.26 us (4%)
    pallas_call x1, Pallas kernels, body(): pl.pallas_call(functools.partial(kernel, (nz, ny, heads, tokens)), out_sh...  57.2 us
    unnamed x1, local copies, waits for them, and re-layouts  2.26 us

profile of v1, /device:TPU:1, one launch (start us, length us, event | category | flops | bytes accessed | tf_op | source)
XLA Modules:
  0.0 59.4 jit_solution(12063319404667952181)
XLA Ops:
  0.0 57.2 %shard_map.55 = bf16[512,1024]{1,0:T(8,128)(2,1)} custom-call(f32[8]{0:T(128)} %gain.1, f32[8]{0:T(128)} %ridge.1, bf16[512,1024]{1,0:T(8,128)(2,1)} %q_hbm.1, bf16[512,1024]{1,0:T(8,128)(2,1)} %k_hbm.1, bf16[512,1024]{1,0:T(8,128)(2,1)} %v_hbm.1), custom_call_target="tpu_custom_call" | custom-call | tf_op jit(solution)/shard_map/pallas_call | solution.py:313
  57.2 2.3 %copy.7 = bf16[512,1024]{1,0:T(8,128)(2,1)} copy(bf16[512,1024]{1,0:T(8,128)(2,1)} %shard_map.55) | data formatting | bytes 2097152

commit v2 on v1

v2 whole, which is shorter than its diff:
```python
import functools

import jax
import jax.numpy as jnp
from jax import lax
from jax.experimental import pallas as pl
from jax.experimental.pallas import tpu as pltpu
from jax.sharding import Mesh
from jax.sharding import PartitionSpec as P

DH = 128
NS_STEPS = 8
REFINE = 2
SEQ = ("seq_0", "seq_1", "seq_2")
MESH = pl.DeviceIdType.MESH
F32, BF16 = jnp.float32, jnp.bfloat16


def dot(a, b):
    return jnp.dot(a, b, preferred_element_type=F32)


def dot_general(a, b, left, right):
    return lax.dot_general(a, b, (((left,), (right,)), ((), ())), preferred_element_type=F32)


def split(x):
    high = x.astype(BF16)
    low = (x - high.astype(F32)).astype(BF16)
    return high, low


def side(x):
    return jnp.concatenate(split(x), axis=1)


def square(x):
    row = side(x)
    return jnp.concatenate([row, row], axis=0)


def fold(p):
    return p[:, :DH] + p[:, DH:]


def iota(shape, dim):
    return lax.broadcasted_iota(jnp.int32, shape, dim)


def pack_gram(gram):
    half = DH // 2
    top, bottom = gram[:half], gram[half:]
    r, c = iota((half, DH), 0), iota((half, DH), 1)
    rolled = pltpu.roll(bottom, half, 1)
    packed = jnp.where((c < half) & (r < c), rolled, top)
    diagonal = jnp.sum(jnp.where(c == r + half, bottom, 0.0), axis=0, keepdims=True)
    return packed, diagonal


def unpack_gram(packed, diagonal):
    half = DH // 2
    r, c = iota((half, DH), 0), iota((half, DH), 1)
    flipped = jnp.concatenate([packed, packed], axis=0).T
    upper_flip, lower_flip = flipped[:half], flipped[half:]
    top = jnp.where((c < half) & (r < c), upper_flip, packed)
    a22 = pltpu.roll(jnp.where(r < c, packed, upper_flip), half, 1)
    bottom = jnp.where(c < half, lower_flip, jnp.where(c == r + half, diagonal, a22))
    return jnp.concatenate([top, bottom], axis=0)


def kernel(
    dims, gain, ridge, q_hbm, k_hbm, v_hbm, o,
    q, k, v, ks, shi, slo, own, state, bcat, ycat, ccat,
    gp, gin, gt, gf, gs, gr, ga, gn, xp, xin, xt, xf, xs, xr, xa, xn,
    load_sem, pair_send, pair_recv, send_sem, recv_sem, span_send, span_recv, ready,
):
    nz, ny, planes, heads, tokens = dims
    groups = nz // planes
    chips = planes * ny
    pieces = 8 * heads
    mine = pieces // 2
    per = mine // chips
    z, y, core = (lax.axis_index(a) for a in SEQ)
    group = z // planes
    chip = (z % planes) * ny + y
    base_piece = core * mine

    def where_is(j):
        return {"seq_0": group * planes + j // ny, "seq_1": j % ny}

    loads = []
    for n, (src, dst) in enumerate(((k_hbm, k), (v_hbm, v), (q_hbm, q))):
        copy = pltpu.make_async_copy(src, dst, load_sem.at[n])
        copy.start()
        loads.append(copy)

    barrier = pltpu.get_barrier_semaphore()
    pl.semaphore_signal(barrier, inc=1, device_id={"seq_2": 1 - core}, device_id_type=MESH)

    @pl.loop(1, chips)
    def _(d):
        pl.semaphore_signal(
            barrier, inc=1, device_id=where_is((chip + d) % chips), device_id_type=MESH
        )

    for n in range(1, groups):

        @pl.when(group + n < groups)
        def _(n=n):
            pl.semaphore_signal(
                barrier, inc=1, device_id={"seq_0": z + n * planes}, device_id_type=MESH
            )

    loads[0].wait()
    loads[1].wait()
    for h in range(heads):
        cols = slice(h * DH, (h + 1) * DH)
        scaled = (k[:, cols].astype(F32) * gain[h]).astype(BF16)
        ks[:, cols] = scaled
        both = dot_general(scaled, jnp.concatenate([scaled, v[:, cols]], axis=1), 0, 0)
        gram, cross = both[:, :DH], both[:, DH:]
        own[h] = gram
        packed, diagonal = pack_gram(gram)
        rows = slice(h * 8, (h + 1) * 8)
        gp[rows, 0:8, :] = packed.reshape(8, 8, DH)
        gp[rows, 8:9, :] = jnp.broadcast_to(diagonal.reshape(1, 1, DH), (8, 1, DH))
        xp[rows] = cross.reshape(8, 16, DH)
    pl.semaphore_wait(barrier, chips + group)
    for n in range(1, groups):

        @pl.when(group >= n)
        def _(n=n):
            pl.semaphore_signal(
                ready.at[n - 1], inc=1, device_id={"seq_0": z - n * planes}, device_id_type=MESH
            )

    def to_partner(src, dst, n):
        return pltpu.make_async_remote_copy(
            src_ref=src, dst_ref=dst, send_sem=pair_send.at[n], recv_sem=pair_recv.at[n],
            device_id={"seq_2": 1 - core}, device_id_type=MESH,
        )

    def to_chip(src, dst, way, there):
        return pltpu.make_async_remote_copy(
            src_ref=src, dst_ref=dst, send_sem=send_sem.at[way], recv_sem=recv_sem.at[way],
            device_id=where_is(there), device_id_type=MESH,
        )

    def slot(ref, j):
        return ref.at[pl.ds(j * per, per)]

    def half_slot(ref, j):
        return ref.at[pl.ds(base_piece + j * per, per)]

    def others(ref):
        return ref.at[pl.ds(0, (chips - 1) * per)]

    def outward(part, came, total, found, way):
        total[...] = part[pl.ds(base_piece, mine)] + came[pl.ds(base_piece, mine)]
        found[pl.ds(chip * per, per)] = total[pl.ds(chip * per, per)]

        @pl.loop(1, chips)
        def _(d):
            there = (chip + d) % chips
            to_chip(slot(total, there), slot(found, chip), way, there).start()

    def span(every, came, way, n):
        return pltpu.make_async_remote_copy(
            src_ref=every.at[pl.ds(0, per)], dst_ref=came.at[pl.ds((n - 1) * per, per)],
            send_sem=span_send.at[way // 2, n - 1], recv_sem=span_recv.at[way // 2, n - 1],
            device_id={"seq_0": z + n * planes}, device_id_type=MESH,
        )

    def homeward(total, found, sums, result, every, came, way):
        to_chip(others(total), others(found), way, chip).wait_recv()
        everything = found[pl.ds(0, per)]
        for j in range(1, chips):
            everything = everything + found[pl.ds(j * per, per)]
        every[pl.ds(0, per)] = everything

        def pass_on():
            for n in range(1, groups):

                @pl.when(group + n < groups)
                def _(n=n):
                    if way == 0:
                        pl.semaphore_wait(ready.at[n - 1], 1)
                    span(every, came, way, n).start()

        pl.when(group > 0)(pass_on)
        every[pl.ds(per, per)] = jnp.zeros_like(everything)
        for n in range(1, groups):

            @pl.when(group >= n)
            def _(n=n):
                span(every, came, way, n).wait_recv()
                every[pl.ds(per, per)] += came[pl.ds((n - 1) * per, per)]

        def body(j, running):
            sums[pl.ds(j * per, per)] = running

            @pl.when(j != chip)
            def _():
                to_chip(slot(sums, j), half_slot(result, chip), way + 1, j).start()

            @pl.when(j == chip)
            def _():
                result[pl.ds(base_piece + chip * per, per)] = running

            return running + found[pl.ds(j * per, per)]

        lax.fori_loop(0, chips, body, every[pl.ds(per, per)])
        pl.when(group == 0)(pass_on)

    def gather(sums, result, way):
        to_chip(others(sums), others(result), way + 1, chip).wait_recv()

    def drain(total, sums, found, result, every, came, way):
        to_chip(others(total), others(found), way, chip).wait_send()
        to_chip(others(sums), others(result), way + 1, chip).wait_send()
        for n in range(1, groups):

            @pl.when(group + n < groups)
            def _(n=n):
                span(every, came, way, n).wait_send()

    def my_half(ref):
        return ref.at[pl.ds(base_piece, mine)]

    gram_pair = to_partner(gp, gin, 0)
    gram_pair.start()
    cross_pair = to_partner(xp, xin, 1)
    cross_pair.start()
    gram_pair.wait_recv()
    outward(gp, gin, gt, gf, 0)
    homeward(gt, gf, gs, gr, ga, gn, 0)
    cross_pair.wait_recv()
    outward(xp, xin, xt, xf, 2)
    gather(gs, gr, 0)
    gram_back = to_partner(my_half(gr), my_half(gr), 2)
    gram_back.start()
    gram_back.wait_recv()

    second = core == 1
    eye = jnp.where(iota((DH, DH), 0) == iota((DH, DH), 1), 1.0, 0.0)
    for h in range(heads):
        rows = slice(h * 8, (h + 1) * 8)
        whole = gr[rows] + jnp.where(second, gin[rows], 0.0)
        prior = unpack_gram(whole[:, 0:8, :].reshape(DH // 2, DH), whole[0, 8:9, :])
        base = prior + ridge[h] * eye
        bcat[h] = square(base)
        end = base + own[h]
        total = jnp.sum(jnp.sum(end * end, axis=1, keepdims=True), axis=0, keepdims=True)
        inverse = 1.0 / jnp.sqrt(total)
        half = end * (0.5 * inverse)
        left = side(half)
        rest = half - fold(dot(left, jnp.concatenate([left, left], axis=0)))
        state[h, :DH] = eye - half
        state[h, DH:] = rest + rest
        own[h] = jnp.broadcast_to(inverse * float(2**NS_STEPS), (DH, DH))

    @pl.loop(1, NS_STEPS - 1)
    def _(step):
        for h in range(heads):
            x = state[h]
            left = side(x)
            row = left[DH:]
            rest = x - fold(dot(left, jnp.concatenate([row, row], axis=0)))
            state[h, :DH] = rest[:DH]
            state[h, DH:] = rest[DH:] + rest[DH:]

    for h in range(heads):
        x = state[h, :DH]
        rest = x - fold(dot(side(x), square(state[h, DH:])))
        ycat[h] = square(rest * own[h])

    loads[2].wait()
    block = 256
    causal = iota((block, block), 0) >= iota((block, block), 1)

    def scores_of(high, keys):
        s = dot_general(high, keys, 1, 1)
        count = keys.shape[0] // block
        if count == 1:
            return jnp.where(causal, s, 0.0).astype(BF16)
        past = s[:, : (count - 1) * block].astype(BF16)
        return jnp.concatenate(
            [past, jnp.where(causal, s[:, (count - 1) * block :], 0.0).astype(BF16)], axis=1
        )

    def columns(h):
        return pl.ds(pl.multiple_of(h * DH, DH), DH)

    def chains_of(pair):
        chains = []
        for r in reversed(range(tokens // block)):
            for which in range(2):
                chains.append((pair * 2 + which, r))
        places = [(slice(r * block, (r + 1) * block), columns(h)) for h, r in chains]
        seen = [(slice(0, (r + 1) * block), columns(h)) for h, r in chains]
        return [h for h, _ in chains], places, seen

    @pl.loop(0, heads // 2)
    def _(pair):
        @pl.when(pair == 1)
        def _():
            homeward(xt, xf, xs, xr, xa, xn, 2)

        hs, places, seen = chains_of(pair)
        query = [q[at] for at in places]
        keys = [ks[at] for at in seen]
        solutions = [fold(dot(x, ycat[h, :DH])) for x, h in zip(query, hs)]
        for repeat in range(REFINE):
            parts = [split(x) for x in solutions]
            scores = [scores_of(x[0], key) for x, key in zip(parts, keys)]
            through = [fold(dot(jnp.concatenate(x, axis=1), bcat[h])) for x, h in zip(parts, hs)]
            in_block = [dot(x, key) for x, key in zip(scores, keys)]
            residual = [
                x.astype(F32) - t - b for x, t, b in zip(query, through, in_block)
            ]
            solutions = [
                x + fold(dot(side(r), ycat[h])) for x, r, h in zip(solutions, residual, hs)
            ]
        for x, at in zip(solutions, places):
            shi[at], slo[at] = split(x)

    gather(xs, xr, 2)
    cross_back = to_partner(my_half(xr), my_half(xr), 3)
    cross_back.start()
    cross_back.wait_recv()
    for h in range(heads):
        rows = slice(h * 8, (h + 1) * 8)
        ccat[h] = square((xr[rows] + jnp.where(second, xin[rows], 0.0)).reshape(DH, DH))

    @pl.loop(0, heads // 2)
    def _(pair):
        hs, places, seen = chains_of(pair)
        high = [shi[at] for at in places]
        scores = [scores_of(x, ks[at]) for x, at in zip(high, seen)]
        past = [
            fold(dot(jnp.concatenate([x, slo[at]], axis=1), ccat[h]))
            for x, at, h in zip(high, places, hs)
        ]
        present = [dot(x, v[at]) for x, at in zip(scores, seen)]
        for a, b, at in zip(past, present, places):
            o[at] = (a + b).astype(BF16)

    drain(gt, gs, gf, gr, ga, gn, 0)
    drain(xt, xs, xf, xr, xa, xn, 2)
    for copy in (gram_pair, cross_pair, gram_back, cross_back):
        copy.wait_send()


def body(dims, query_rows, key_rows, value_rows, key_gain, regularizer):
    tokens, width = query_rows.shape
    heads = key_gain.shape[0]
    nz, ny, planes = dims
    chips = planes * ny
    groups = nz // planes
    pieces = 8 * heads
    mine = pieces // 2
    per = mine // chips
    rows = pltpu.VMEM((tokens, width), BF16)

    def exchange(depth):
        whole = pltpu.VMEM((pieces, depth, DH), F32)
        half = pltpu.VMEM((mine, depth, DH), F32)
        sums = pltpu.VMEM((2 * per, depth, DH), F32)
        came = pltpu.VMEM(((groups - 1) * per, depth, DH), F32)
        return [whole, whole, half, half, half, whole, sums, came]

    cat = pltpu.VMEM((heads, 2 * DH, 2 * DH), BF16)
    return pl.pallas_call(
        functools.partial(kernel, (nz, ny, planes, heads, tokens)),
        out_shape=pltpu.VMEM((tokens, width), BF16),
        in_specs=[pl.BlockSpec(memory_space=pltpu.SMEM)] * 2
        + [pl.BlockSpec(memory_space=pl.ANY)] * 3,
        out_specs=pl.BlockSpec(memory_space=pltpu.VMEM),
        scratch_shapes=[rows] * 6
        + [pltpu.VMEM((heads, DH, DH), F32), pltpu.VMEM((heads, 2 * DH, DH), F32), cat, cat, cat]
        + exchange(9)
        + exchange(16)
        + [
            pltpu.SemaphoreType.DMA((3,)),
            pltpu.SemaphoreType.DMA((4,)),
            pltpu.SemaphoreType.DMA((4,)),
            pltpu.SemaphoreType.DMA((4,)),
            pltpu.SemaphoreType.DMA((4,)),
            pltpu.SemaphoreType.DMA((2, groups - 1)),
            pltpu.SemaphoreType.DMA((2, groups - 1)),
            pltpu.SemaphoreType.REGULAR((groups - 1,)),
        ],
        compiler_params=pltpu.CompilerParams(collective_id=0, has_side_effects=True),
    )(key_gain, regularizer, query_rows, key_rows, value_rows)


def solution(mesh):
    nz, ny, cores, planes = 8, 4, 2, 2
    torus = Mesh(
        mesh.devices.reshape(nz, ny, cores, mesh.shape["head"]), SEQ + ("head",)
    )
    in_specs = (P(SEQ, "head"), P(SEQ, "head"), P(SEQ, "head"), P("head"), P("head"))
    return jax.shard_map(
        functools.partial(body, (nz, ny, planes)), mesh=torus, in_specs=in_specs,
        out_specs=P(SEQ, "head"), check_vma=False,
    )
```

time: 59.6 us -> 40.5 us (0.68)
  the two profiles are of different devices: /device:TPU:1 before, /device:TPU:225 now
where the time goes in v2:
time: 40.5 us; the launch traced here: 40.4 us
  Pallas kernels  39.4 us (97%)
  local copies, waits for them, and re-layouts  0.97 us (2%)
    pallas_call x1, Pallas kernels, body(): pl.pallas_call(functools.partial(kernel, (nz, ny, planes, heads, tokens))...  39.4 us
    unnamed x1, local copies, waits for them, and re-layouts  0.97 us

profile of v2, /device:TPU:225, one launch (start us, length us, event | category | flops | bytes accessed | tf_op | source)
XLA Modules:
  0.0 40.4 jit_solution(14651698686832097940)
XLA Ops:
  0.0 39.4 %shard_map.55 = bf16[512,1024]{1,0:T(8,128)(2,1)S(1)} custom-call(f32[8]{0:T(128)} %gain.1, f32[8]{0:T(128)} %ridge.1, bf16[512,1024]{1,0:T(8,128)(2,1)} %q_hbm.1, bf16[512,1024]{1,0:T(8,128)(2,1)} %k_hbm.1, bf16[512,1024]{1,0:T(8,128)(2,1)} %v_hbm.1), custom_call_target="tpu_custom_call" | custom-call | tf_op jit(solution)/shard_map/pallas_call | solution.py:373
  39.4 1.0 %copy.7 = bf16[512,1024]{1,0:T(8,128)(2,1)} copy(bf16[512,1024]{1,0:T(8,128)(2,1)S(1)} %shard_map.55) | data formatting | bytes 2097152

commit v3 on v2

--- a/solution.py
+++ b/solution.py
@@ -69,8 +69,8 @@
 
 
 def kernel(
-    dims, gain, ridge, q_hbm, k_hbm, v_hbm, o,
-    q, k, v, ks, shi, slo, own, state, bcat, ycat, ccat,
+    dims, gain_hbm, ridge_hbm, q_hbm, k_hbm, v_hbm, o,
+    gain, ridge, q, k, v, ks, shi, slo, own, state, bcat, ycat, ccat,
     gp, gin, gt, gf, gs, gr, ga, gn, xp, xin, xt, xf, xs, xr, xa, xn,
     load_sem, pair_send, pair_recv, send_sem, recv_sem, span_send, span_recv, ready,
 ):
@@ -88,12 +88,6 @@
     def where_is(j):
         return {"seq_0": group * planes + j // ny, "seq_1": j % ny}
 
-    loads = []
-    for n, (src, dst) in enumerate(((k_hbm, k), (v_hbm, v), (q_hbm, q))):
-        copy = pltpu.make_async_copy(src, dst, load_sem.at[n])
-        copy.start()
-        loads.append(copy)
-
     barrier = pltpu.get_barrier_semaphore()
     pl.semaphore_signal(barrier, inc=1, device_id={"seq_2": 1 - core}, device_id_type=MESH)
 
@@ -111,8 +105,14 @@
                 barrier, inc=1, device_id={"seq_0": z + n * planes}, device_id_type=MESH
             )
 
-    loads[0].wait()
-    loads[1].wait()
+    loads = []
+    for n, (src, dst) in enumerate(((gain_hbm, gain), (k_hbm, k), (v_hbm, v), (ridge_hbm, ridge), (q_hbm, q))):
+        copy = pltpu.make_async_copy(src, dst, load_sem.at[n])
+        copy.start()
+        loads.append(copy)
+
+    for n in range(3):
+        loads[n].wait()
     for h in range(heads):
         cols = slice(h * DH, (h + 1) * DH)
         scaled = (k[:, cols].astype(F32) * gain[h]).astype(BF16)
@@ -171,24 +171,24 @@
             device_id={"seq_0": z + n * planes}, device_id_type=MESH,
         )
 
-    def homeward(total, found, sums, result, every, came, way):
+    def pass_on(every, came, way):
+        for n in range(1, groups):
+
+            @pl.when(group + n < groups)
+            def _(n=n):
+                if way == 0:
+                    pl.semaphore_wait(ready.at[n - 1], 1)
+                span(every, came, way, n).start()
+
+    def collect(total, found, every, way):
         to_chip(others(total), others(found), way, chip).wait_recv()
         everything = found[pl.ds(0, per)]
         for j in range(1, chips):
             everything = everything + found[pl.ds(j * per, per)]
         every[pl.ds(0, per)] = everything
 
-        def pass_on():
-            for n in range(1, groups):
-
-                @pl.when(group + n < groups)
-                def _(n=n):
-                    if way == 0:
-                        pl.semaphore_wait(ready.at[n - 1], 1)
-                    span(every, came, way, n).start()
-
-        pl.when(group > 0)(pass_on)
-        every[pl.ds(per, per)] = jnp.zeros_like(everything)
+    def homeward(found, sums, result, every, came, way):
+        every[pl.ds(per, per)] = jnp.zeros((per,) + found.shape[1:], F32)
         for n in range(1, groups):
 
             @pl.when(group >= n)
@@ -210,7 +210,6 @@
             return running + found[pl.ds(j * per, per)]
 
         lax.fori_loop(0, chips, body, every[pl.ds(per, per)])
-        pl.when(group == 0)(pass_on)
 
     def gather(sums, result, way):
         to_chip(others(sums), others(result), way + 1, chip).wait_recv()
@@ -227,22 +226,43 @@
     def my_half(ref):
         return ref.at[pl.ds(base_piece, mine)]
 
-    gram_pair = to_partner(gp, gin, 0)
+    def other_half(ref):
+        return ref.at[pl.ds(mine - base_piece, mine)]
+
+    gram_pair = to_partner(other_half(gp), other_half(gin), 0)
     gram_pair.start()
+    gram_rest = to_partner(my_half(gp), my_half(gin), 4)
+    gram_rest.start()
     cross_pair = to_partner(xp, xin, 1)
     cross_pair.start()
     gram_pair.wait_recv()
     outward(gp, gin, gt, gf, 0)
-    homeward(gt, gf, gs, gr, ga, gn, 0)
     cross_pair.wait_recv()
     outward(xp, xin, xt, xf, 2)
+    collect(gt, gf, ga, 0)
+
+    @pl.when(group > 0)
+    def _():
+        pass_on(ga, gn, 0)
+
+    homeward(gf, gs, gr, ga, gn, 0)
+
+    @pl.when(group == 0)
+    def _():
+        pass_on(ga, gn, 0)
+
+    collect(xt, xf, xa, 2)
+    pass_on(xa, xn, 2)
     gather(gs, gr, 0)
     gram_back = to_partner(my_half(gr), my_half(gr), 2)
     gram_back.start()
+    gram_rest.wait_recv()
+    loads[3].wait()
     gram_back.wait_recv()
 
     second = core == 1
     eye = jnp.where(iota((DH, DH), 0) == iota((DH, DH), 1), 1.0, 0.0)
+    inverses = []
     for h in range(heads):
         rows = slice(h * 8, (h + 1) * 8)
         whole = gr[rows] + jnp.where(second, gin[rows], 0.0)
@@ -250,14 +270,19 @@
         base = prior + ridge[h] * eye
         bcat[h] = square(base)
         end = base + own[h]
-        total = jnp.sum(jnp.sum(end * end, axis=1, keepdims=True), axis=0, keepdims=True)
-        inverse = 1.0 / jnp.sqrt(total)
-        half = end * (0.5 * inverse)
+        own[h] = end
+        total = jnp.sum(jnp.sum(end * end, axis=0, keepdims=True), axis=1, keepdims=True)
+        inverses.append(1.0 / jnp.sqrt(total))
+    for h in range(heads):
+        half = own[h] * (0.5 * inverses[h])
         left = side(half)
         rest = half - fold(dot(left, jnp.concatenate([left, left], axis=0)))
         state[h, :DH] = eye - half
         state[h, DH:] = rest + rest
-        own[h] = jnp.broadcast_to(inverse * float(2**NS_STEPS), (DH, DH))
+    for h in range(heads):
+        own[h] = jnp.broadcast_to(inverses[h] * float(2**NS_STEPS), (DH, DH))
+
+    homeward(xf, xs, xr, xa, xn, 2)
 
     @pl.loop(1, NS_STEPS - 1)
     def _(step):
@@ -274,7 +299,7 @@
         rest = x - fold(dot(side(x), square(state[h, DH:])))
         ycat[h] = square(rest * own[h])
 
-    loads[2].wait()
+    loads[4].wait()
     block = 256
     causal = iota((block, block), 0) >= iota((block, block), 1)
 
@@ -300,11 +325,14 @@
         seen = [(slice(0, (r + 1) * block), columns(h)) for h, r in chains]
         return [h for h, _ in chains], places, seen
 
+    cross_back = to_partner(my_half(xr), my_half(xr), 3)
+
     @pl.loop(0, heads // 2)
     def _(pair):
-        @pl.when(pair == 1)
+        @pl.when(pair == heads // 2 - 2)
         def _():
-            homeward(xt, xf, xs, xr, xa, xn, 2)
+            gather(xs, xr, 2)
+            cross_back.start()
 
         hs, places, seen = chains_of(pair)
         query = [q[at] for at in places]
@@ -324,9 +352,6 @@
         for x, at in zip(solutions, places):
             shi[at], slo[at] = split(x)
 
-    gather(xs, xr, 2)
-    cross_back = to_partner(my_half(xr), my_half(xr), 3)
-    cross_back.start()
     cross_back.wait_recv()
     for h in range(heads):
         rows = slice(h * 8, (h + 1) * 8)
@@ -347,7 +372,7 @@
 
     drain(gt, gs, gf, gr, ga, gn, 0)
     drain(xt, xs, xf, xr, xa, xn, 2)
-    for copy in (gram_pair, cross_pair, gram_back, cross_back):
+    for copy in (gram_pair, gram_rest, cross_pair, gram_back, cross_back):
         copy.wait_send()
 
 
@@ -373,17 +398,17 @@
     return pl.pallas_call(
         functools.partial(kernel, (nz, ny, planes, heads, tokens)),
         out_shape=pltpu.VMEM((tokens, width), BF16),
-        in_specs=[pl.BlockSpec(memory_space=pltpu.SMEM)] * 2
-        + [pl.BlockSpec(memory_space=pl.ANY)] * 3,
+        in_specs=[pl.BlockSpec(memory_space=pl.ANY)] * 5,
         out_specs=pl.BlockSpec(memory_space=pltpu.VMEM),
-        scratch_shapes=[rows] * 6
+        scratch_shapes=[pltpu.SMEM((heads,), F32)] * 2
+        + [rows] * 6
         + [pltpu.VMEM((heads, DH, DH), F32), pltpu.VMEM((heads, 2 * DH, DH), F32), cat, cat, cat]
         + exchange(9)
         + exchange(16)
         + [
-            pltpu.SemaphoreType.DMA((3,)),
-            pltpu.SemaphoreType.DMA((4,)),
-            pltpu.SemaphoreType.DMA((4,)),
+            pltpu.SemaphoreType.DMA((5,)),
+            pltpu.SemaphoreType.DMA((5,)),
+            pltpu.SemaphoreType.DMA((5,)),
             pltpu.SemaphoreType.DMA((4,)),
             pltpu.SemaphoreType.DMA((4,)),
             pltpu.SemaphoreType.DMA((2, groups - 1)),

time: 40.5 us -> 34.7 us (0.86)
  Pallas kernels: 39.4 us -> 33.6 us
    pallas_call x1, Pallas kernels: 39.4 us -> 33.6 us  [body(): pl.pallas_call(functools.partial(kernel, (nz, ny, planes, heads, tokens))...]
where the time goes in v3:
time: 34.7 us; the launch traced here: 34.6 us
  Pallas kernels  33.6 us (97%)
  local copies, waits for them, and re-layouts  0.97 us (3%)
    pallas_call x1, Pallas kernels, body(): pl.pallas_call(functools.partial(kernel, (nz, ny, planes, heads, tokens))...  33.6 us
    unnamed x1, local copies, waits for them, and re-layouts  0.97 us

profile of v3, /device:TPU:225, one launch (start us, length us, event | category | flops | bytes accessed | tf_op | source)
XLA Modules:
  0.0 34.6 jit_solution(1483189154044318601)
XLA Ops:
  0.0 33.6 %shard_map.55 = bf16[512,1024]{1,0:T(8,128)(2,1)S(1)} custom-call(f32[8]{0:T(128)} %gain_hbm.1, f32[8]{0:T(128)} %ridge_hbm.1, bf16[512,1024]{1,0:T(8,128)(2,1)} %q_hbm.1, bf16[512,1024]{1,0:T(8,128)(2,1)} %k_hbm.1, bf16[512,1024]{1,0:T(8,128)(2,1)} %v_hbm.1), custom_call_target="tpu_custom_call" | custom-call | tf_op jit(solution)/shard_map/pallas_call | solution.py:398
  33.6 1.0 %copy.7 = bf16[512,1024]{1,0:T(8,128)(2,1)} copy(bf16[512,1024]{1,0:T(8,128)(2,1)S(1)} %shard_map.55) | data formatting | bytes 2097152

commit v4 on v3

--- a/solution.py
+++ b/solution.py
@@ -63,7 +63,7 @@
     flipped = jnp.concatenate([packed, packed], axis=0).T
     upper_flip, lower_flip = flipped[:half], flipped[half:]
     top = jnp.where((c < half) & (r < c), upper_flip, packed)
-    a22 = pltpu.roll(jnp.where(r < c, packed, upper_flip), half, 1)
+    a22 = jnp.where(c > r + half, pltpu.roll(packed, half, 1), upper_flip)
     bottom = jnp.where(c < half, lower_flip, jnp.where(c == r + half, diagonal, a22))
     return jnp.concatenate([top, bottom], axis=0)
 
@@ -88,6 +88,10 @@
     def where_is(j):
         return {"seq_0": group * planes + j // ny, "seq_1": j % ny}
 
+    steps = [(a, b) for a in range(planes) for b in range(ny) if a or b]
+    steps.sort(key=lambda s: -(s[0] + min(s[1], ny - s[1])))
+    others_at = [((z + a) % planes) * ny + (y + b) % ny for a, b in steps]
+
     barrier = pltpu.get_barrier_semaphore()
     pl.semaphore_signal(barrier, inc=1, device_id={"seq_2": 1 - core}, device_id_type=MESH)
 
@@ -106,33 +110,33 @@
             )
 
     loads = []
-    for n, (src, dst) in enumerate(((gain_hbm, gain), (k_hbm, k), (v_hbm, v), (ridge_hbm, ridge), (q_hbm, q))):
+    moves = [(gain_hbm, gain)]
+    for first in (1 - core, core):
+        cols = pl.ds(pl.multiple_of(first * (heads // 2 * DH), DH), heads // 2 * DH)
+        moves += [(k_hbm.at[:, cols], k.at[:, cols]), (v_hbm.at[:, cols], v.at[:, cols])]
+    moves += [(ridge_hbm, ridge), (q_hbm, q)]
+    for n, (src, dst) in enumerate(moves):
         copy = pltpu.make_async_copy(src, dst, load_sem.at[n])
         copy.start()
         loads.append(copy)
 
-    for n in range(3):
-        loads[n].wait()
-    for h in range(heads):
-        cols = slice(h * DH, (h + 1) * DH)
-        scaled = (k[:, cols].astype(F32) * gain[h]).astype(BF16)
-        ks[:, cols] = scaled
-        both = dot_general(scaled, jnp.concatenate([scaled, v[:, cols]], axis=1), 0, 0)
-        gram, cross = both[:, :DH], both[:, DH:]
-        own[h] = gram
-        packed, diagonal = pack_gram(gram)
-        rows = slice(h * 8, (h + 1) * 8)
-        gp[rows, 0:8, :] = packed.reshape(8, 8, DH)
-        gp[rows, 8:9, :] = jnp.broadcast_to(diagonal.reshape(1, 1, DH), (8, 1, DH))
-        xp[rows] = cross.reshape(8, 16, DH)
-    pl.semaphore_wait(barrier, chips + group)
-    for n in range(1, groups):
-
-        @pl.when(group >= n)
-        def _(n=n):
-            pl.semaphore_signal(
-                ready.at[n - 1], inc=1, device_id={"seq_0": z - n * planes}, device_id_type=MESH
-            )
+    def columns(h):
+        return pl.ds(pl.multiple_of(h * DH, DH), DH)
+
+    def states(first):
+        for n in range(heads // 2):
+            h = first + n
+            cols = columns(h)
+            scaled = (k[:, cols].astype(F32) * gain[h]).astype(BF16)
+            ks[:, cols] = scaled
+            both = dot_general(scaled, jnp.concatenate([scaled, v[:, cols]], axis=1), 0, 0)
+            gram, cross = both[:, :DH], both[:, DH:]
+            own[h] = gram
+            packed, diagonal = pack_gram(gram)
+            rows = pl.ds(h * 8, 8)
+            gp[rows, 0:8, :] = packed.reshape(8, 8, DH)
+            gp[rows, 8:9, :] = jnp.broadcast_to(diagonal.reshape(1, 1, DH), (8, 1, DH))
+            xp[rows] = cross.reshape(8, 16, DH)
 
     def to_partner(src, dst, n):
         return pltpu.make_async_remote_copy(
@@ -159,9 +163,7 @@
         total[...] = part[pl.ds(base_piece, mine)] + came[pl.ds(base_piece, mine)]
         found[pl.ds(chip * per, per)] = total[pl.ds(chip * per, per)]
 
-        @pl.loop(1, chips)
-        def _(d):
-            there = (chip + d) % chips
+        for there in others_at:
             to_chip(slot(total, there), slot(found, chip), way, there).start()
 
     def span(every, came, way, n):
@@ -196,20 +198,13 @@
                 span(every, came, way, n).wait_recv()
                 every[pl.ds(per, per)] += came[pl.ds((n - 1) * per, per)]
 
-        def body(j, running):
+        running = every[pl.ds(per, per)]
+        for j in range(chips):
             sums[pl.ds(j * per, per)] = running
-
-            @pl.when(j != chip)
-            def _():
-                to_chip(slot(sums, j), half_slot(result, chip), way + 1, j).start()
-
-            @pl.when(j == chip)
-            def _():
-                result[pl.ds(base_piece + chip * per, per)] = running
-
-            return running + found[pl.ds(j * per, per)]
-
-        lax.fori_loop(0, chips, body, every[pl.ds(per, per)])
+            running = running + found[pl.ds(j * per, per)]
+        for there in others_at:
+            to_chip(slot(sums, there), half_slot(result, chip), way + 1, there).start()
+        result[pl.ds(base_piece + chip * per, per)] = sums[pl.ds(chip * per, per)]
 
     def gather(sums, result, way):
         to_chip(others(sums), others(result), way + 1, chip).wait_recv()
@@ -229,12 +224,29 @@
     def other_half(ref):
         return ref.at[pl.ds(mine - base_piece, mine)]
 
+    for n in range(3):
+        loads[n].wait()
+    states((1 - core) * (heads // 2))
+    pl.semaphore_wait(barrier, chips + group)
     gram_pair = to_partner(other_half(gp), other_half(gin), 0)
     gram_pair.start()
+    cross_pair = to_partner(other_half(xp), other_half(xin), 1)
+    cross_pair.start()
+    for n in range(1, groups):
+
+        @pl.when(group >= n)
+        def _(n=n):
+            pl.semaphore_signal(
+                ready.at[n - 1], inc=1, device_id={"seq_0": z - n * planes}, device_id_type=MESH
+            )
+
+    for n in range(3, 5):
+        loads[n].wait()
+    states(core * (heads // 2))
     gram_rest = to_partner(my_half(gp), my_half(gin), 4)
     gram_rest.start()
-    cross_pair = to_partner(xp, xin, 1)
-    cross_pair.start()
+    cross_rest = to_partner(my_half(xp), my_half(xin), 5)
+    cross_rest.start()
     gram_pair.wait_recv()
     outward(gp, gin, gt, gf, 0)
     cross_pair.wait_recv()
@@ -257,49 +269,48 @@
     gram_back = to_partner(my_half(gr), my_half(gr), 2)
     gram_back.start()
     gram_rest.wait_recv()
-    loads[3].wait()
-    gram_back.wait_recv()
+    loads[-2].wait()
 
     second = core == 1
     eye = jnp.where(iota((DH, DH), 0) == iota((DH, DH), 1), 1.0, 0.0)
-    inverses = []
-    for h in range(heads):
-        rows = slice(h * 8, (h + 1) * 8)
-        whole = gr[rows] + jnp.where(second, gin[rows], 0.0)
-        prior = unpack_gram(whole[:, 0:8, :].reshape(DH // 2, DH), whole[0, 8:9, :])
-        base = prior + ridge[h] * eye
-        bcat[h] = square(base)
-        end = base + own[h]
-        own[h] = end
-        total = jnp.sum(jnp.sum(end * end, axis=0, keepdims=True), axis=1, keepdims=True)
-        inverses.append(1.0 / jnp.sqrt(total))
-    for h in range(heads):
-        half = own[h] * (0.5 * inverses[h])
-        left = side(half)
-        rest = half - fold(dot(left, jnp.concatenate([left, left], axis=0)))
-        state[h, :DH] = eye - half
-        state[h, DH:] = rest + rest
-    for h in range(heads):
-        own[h] = jnp.broadcast_to(inverses[h] * float(2**NS_STEPS), (DH, DH))
+    def matrices(first):
+        for n in range(heads // 2):
+            h = first + n
+            rows = pl.ds(h * 8, 8)
+            whole = gr[rows] + jnp.where(second, gin[rows], 0.0)
+            prior = unpack_gram(whole[:, 0:8, :].reshape(DH // 2, DH), whole[0, 8:9, :])
+            base = prior + ridge[h] * eye
+            bcat[h] = square(base)
+            end = base + own[h]
+            total = jnp.sum(jnp.sum(end * end, axis=0, keepdims=True), axis=1, keepdims=True)
+            inverse = 1.0 / jnp.sqrt(total)
+            left = side(end)
+            squared = fold(dot(left, jnp.concatenate([left, left], axis=0)))
+            half = end * (0.5 * inverse)
+            state[h, :DH] = eye - half
+            state[h, DH:] = half + half - squared * (0.5 * inverse * inverse)
+            own[h] = jnp.broadcast_to(inverse * float(2**NS_STEPS), (DH, DH))
+
+    matrices(core * (heads // 2))
+    gram_back.wait_recv()
+    matrices((1 - core) * (heads // 2))
 
     homeward(xf, xs, xr, xa, xn, 2)
 
-    @pl.loop(1, NS_STEPS - 1)
-    def _(step):
-        for h in range(heads):
-            x = state[h]
-            left = side(x)
-            row = left[DH:]
-            rest = x - fold(dot(left, jnp.concatenate([row, row], axis=0)))
-            state[h, :DH] = rest[:DH]
-            state[h, DH:] = rest[DH:] + rest[DH:]
+    for h in [*range(heads)] * (NS_STEPS - 2):
+        x = state[h]
+        left = side(x)
+        row = left[DH:]
+        rest = x - fold(dot(left, jnp.concatenate([row, row], axis=0)))
+        state[h, :DH] = rest[:DH]
+        state[h, DH:] = rest[DH:] + rest[DH:]
 
     for h in range(heads):
         x = state[h, :DH]
         rest = x - fold(dot(side(x), square(state[h, DH:])))
         ycat[h] = square(rest * own[h])
 
-    loads[4].wait()
+    loads[-1].wait()
     block = 256
     causal = iota((block, block), 0) >= iota((block, block), 1)
 
@@ -313,23 +324,25 @@
             [past, jnp.where(causal, s[:, (count - 1) * block :], 0.0).astype(BF16)], axis=1
         )
 
-    def columns(h):
-        return pl.ds(pl.multiple_of(h * DH, DH), DH)
+    def mixed(scores, rows, parts, matrix):
+        left = jnp.concatenate([scores, *parts], axis=1)
+        padded = jnp.concatenate([rows, jnp.zeros_like(rows)], axis=1)
+        return fold(dot(left, jnp.concatenate([padded, matrix], axis=0)))
 
     def chains_of(pair):
         chains = []
         for r in reversed(range(tokens // block)):
-            for which in range(2):
-                chains.append((pair * 2 + which, r))
+            for which in range(4):
+                chains.append((pair * 4 + which, r))
         places = [(slice(r * block, (r + 1) * block), columns(h)) for h, r in chains]
         seen = [(slice(0, (r + 1) * block), columns(h)) for h, r in chains]
         return [h for h, _ in chains], places, seen
 
     cross_back = to_partner(my_half(xr), my_half(xr), 3)
 
-    @pl.loop(0, heads // 2)
+    @pl.loop(0, heads // 4)
     def _(pair):
-        @pl.when(pair == heads // 2 - 2)
+        @pl.when(pair == 1)
         def _():
             gather(xs, xr, 2)
             cross_back.start()
@@ -341,10 +354,9 @@
         for repeat in range(REFINE):
             parts = [split(x) for x in solutions]
             scores = [scores_of(x[0], key) for x, key in zip(parts, keys)]
-            through = [fold(dot(jnp.concatenate(x, axis=1), bcat[h])) for x, h in zip(parts, hs)]
-            in_block = [dot(x, key) for x, key in zip(scores, keys)]
             residual = [
-                x.astype(F32) - t - b for x, t, b in zip(query, through, in_block)
+                x.astype(F32) - mixed(c, key, part, bcat[h])
+                for x, c, key, part, h in zip(query, scores, keys, parts, hs)
             ]
             solutions = [
                 x + fold(dot(side(r), ycat[h])) for x, r, h in zip(solutions, residual, hs)
@@ -352,27 +364,23 @@
         for x, at in zip(solutions, places):
             shi[at], slo[at] = split(x)
 
+    cross_rest.wait_recv()
     cross_back.wait_recv()
     for h in range(heads):
         rows = slice(h * 8, (h + 1) * 8)
         ccat[h] = square((xr[rows] + jnp.where(second, xin[rows], 0.0)).reshape(DH, DH))
 
-    @pl.loop(0, heads // 2)
+    @pl.loop(0, heads // 4)
     def _(pair):
         hs, places, seen = chains_of(pair)
         high = [shi[at] for at in places]
         scores = [scores_of(x, ks[at]) for x, at in zip(high, seen)]
-        past = [
-            fold(dot(jnp.concatenate([x, slo[at]], axis=1), ccat[h]))
-            for x, at, h in zip(high, places, hs)
-        ]
-        present = [dot(x, v[at]) for x, at in zip(scores, seen)]
-        for a, b, at in zip(past, present, places):
-            o[at] = (a + b).astype(BF16)
+        for x, c, at, there, h in zip(high, scores, places, seen, hs):
+            o[at] = mixed(c, v[there], (x, slo[at]), ccat[h]).astype(BF16)
 
     drain(gt, gs, gf, gr, ga, gn, 0)
     drain(xt, xs, xf, xr, xa, xn, 2)
-    for copy in (gram_pair, gram_rest, cross_pair, gram_back, cross_back):
+    for copy in (gram_pair, gram_rest, cross_pair, cross_rest, gram_back, cross_back):
         copy.wait_send()
 
 
@@ -406,9 +414,9 @@
         + exchange(9)
         + exchange(16)
         + [
-            pltpu.SemaphoreType.DMA((5,)),
-            pltpu.SemaphoreType.DMA((5,)),
-            pltpu.SemaphoreType.DMA((5,)),
+            pltpu.SemaphoreType.DMA((7,)),
+            pltpu.SemaphoreType.DMA((6,)),
+            pltpu.SemaphoreType.DMA((6,)),
             pltpu.SemaphoreType.DMA((4,)),
             pltpu.SemaphoreType.DMA((4,)),
             pltpu.SemaphoreType.DMA((2, groups - 1)),

time: 34.7 us -> 32.3 us (0.931)
  Pallas kernels: 33.6 us -> 31.2 us
    pallas_call x1, Pallas kernels: 33.6 us -> 31.2 us  [body(): pl.pallas_call(functools.partial(kernel, (nz, ny, planes, heads, tokens))...]
where the time goes in v4:
time: 32.3 us; the launch traced here: 32.2 us
  Pallas kernels  31.2 us (97%)
  local copies, waits for them, and re-layouts  0.97 us (3%)
    pallas_call x1, Pallas kernels, body(): pl.pallas_call(functools.partial(kernel, (nz, ny, planes, heads, tokens))...  31.2 us
    unnamed x1, local copies, waits for them, and re-layouts  0.97 us

profile of v4, /device:TPU:225, one launch (start us, length us, event | category | flops | bytes accessed | tf_op | source)
XLA Modules:
  0.0 32.2 jit_solution(14590397879473874338)
XLA Ops:
  0.0 31.2 %shard_map.55 = bf16[512,1024]{1,0:T(8,128)(2,1)S(1)} custom-call(f32[8]{0:T(128)} %gain_hbm.1, f32[8]{0:T(128)} %ridge_hbm.1, bf16[512,1024]{1,0:T(8,128)(2,1)} %q_hbm.1, bf16[512,1024]{1,0:T(8,128)(2,1)} %k_hbm.1, bf16[512,1024]{1,0:T(8,128)(2,1)} %v_hbm.1), custom_call_target="tpu_custom_call" | custom-call | tf_op jit(solution)/shard_map/pallas_call | solution.py:406
  31.2 1.0 %copy.7 = bf16[512,1024]{1,0:T(8,128)(2,1)} copy(bf16[512,1024]{1,0:T(8,128)(2,1)S(1)} %shard_map.55) | data formatting | bytes 2097152

commit v5 on v4

--- a/solution.py
+++ b/solution.py
@@ -77,7 +77,7 @@
     nz, ny, planes, heads, tokens = dims
     groups = nz // planes
     chips = planes * ny
-    pieces = 8 * heads
+    pieces = 2 * heads
     mine = pieces // 2
     per = mine // chips
     z, y, core = (lax.axis_index(a) for a in SEQ)
@@ -95,10 +95,9 @@
     barrier = pltpu.get_barrier_semaphore()
     pl.semaphore_signal(barrier, inc=1, device_id={"seq_2": 1 - core}, device_id_type=MESH)
 
-    @pl.loop(1, chips)
-    def _(d):
+    for there in others_at:
         pl.semaphore_signal(
-            barrier, inc=1, device_id=where_is((chip + d) % chips), device_id_type=MESH
+            barrier, inc=1, device_id=where_is(there), device_id_type=MESH
         )
 
     for n in range(1, groups):
@@ -133,10 +132,10 @@
             gram, cross = both[:, :DH], both[:, DH:]
             own[h] = gram
             packed, diagonal = pack_gram(gram)
-            rows = pl.ds(h * 8, 8)
-            gp[rows, 0:8, :] = packed.reshape(8, 8, DH)
-            gp[rows, 8:9, :] = jnp.broadcast_to(diagonal.reshape(1, 1, DH), (8, 1, DH))
-            xp[rows] = cross.reshape(8, 16, DH)
+            rows = pl.ds(h * 2, 2)
+            gp[rows, 0:32, :] = packed.reshape(2, 32, DH)
+            gp[rows, 32:33, :] = jnp.broadcast_to(diagonal.reshape(1, 1, DH), (2, 1, DH))
+            xp[rows] = cross.reshape(2, 64, DH)
 
     def to_partner(src, dst, n):
         return pltpu.make_async_remote_copy(
@@ -173,8 +172,8 @@
             device_id={"seq_0": z + n * planes}, device_id_type=MESH,
         )
 
-    def pass_on(every, came, way):
-        for n in range(1, groups):
+    def pass_on(every, came, way, first=1, last=None):
+        for n in range(first, groups if last is None else last):
 
             @pl.when(group + n < groups)
             def _(n=n):
@@ -276,9 +275,9 @@
     def matrices(first):
         for n in range(heads // 2):
             h = first + n
-            rows = pl.ds(h * 8, 8)
+            rows = pl.ds(h * 2, 2)
             whole = gr[rows] + jnp.where(second, gin[rows], 0.0)
-            prior = unpack_gram(whole[:, 0:8, :].reshape(DH // 2, DH), whole[0, 8:9, :])
+            prior = unpack_gram(whole[:, 0:32, :].reshape(DH // 2, DH), whole[0, 32:33, :])
             base = prior + ridge[h] * eye
             bcat[h] = square(base)
             end = base + own[h]
@@ -367,7 +366,7 @@
     cross_rest.wait_recv()
     cross_back.wait_recv()
     for h in range(heads):
-        rows = slice(h * 8, (h + 1) * 8)
+        rows = slice(h * 2, (h + 1) * 2)
         ccat[h] = square((xr[rows] + jnp.where(second, xin[rows], 0.0)).reshape(DH, DH))
 
     @pl.loop(0, heads // 4)
@@ -390,7 +389,7 @@
     nz, ny, planes = dims
     chips = planes * ny
     groups = nz // planes
-    pieces = 8 * heads
+    pieces = 2 * heads
     mine = pieces // 2
     per = mine // chips
     rows = pltpu.VMEM((tokens, width), BF16)
@@ -411,8 +410,8 @@
         scratch_shapes=[pltpu.SMEM((heads,), F32)] * 2
         + [rows] * 6
         + [pltpu.VMEM((heads, DH, DH), F32), pltpu.VMEM((heads, 2 * DH, DH), F32), cat, cat, cat]
-        + exchange(9)
-        + exchange(16)
+        + exchange(33)
+        + exchange(64)
         + [
             pltpu.SemaphoreType.DMA((7,)),
             pltpu.SemaphoreType.DMA((6,)),

time: 32.3 us -> 32 us (level)
  no operation moved by 1% of the time
where the time goes in v5:
time: 32 us; the launch traced here: 31.9 us
  Pallas kernels  30.9 us (97%)
  local copies, waits for them, and re-layouts  0.97 us (3%)
    pallas_call x1, Pallas kernels, body(): pl.pallas_call(functools.partial(kernel, (nz, ny, planes, heads, tokens))...  30.9 us
    unnamed x1, local copies, waits for them, and re-layouts  0.97 us

profile of v5, /device:TPU:225, one launch (start us, length us, event | category | flops | bytes accessed | tf_op | source)
XLA Modules:
  0.0 31.9 jit_solution(17693238464860427151)
XLA Ops:
  0.0 30.9 %shard_map.55 = bf16[512,1024]{1,0:T(8,128)(2,1)S(1)} custom-call(f32[8]{0:T(128)} %gain_hbm.1, f32[8]{0:T(128)} %ridge_hbm.1, bf16[512,1024]{1,0:T(8,128)(2,1)} %q_hbm.1, bf16[512,1024]{1,0:T(8,128)(2,1)} %k_hbm.1, bf16[512,1024]{1,0:T(8,128)(2,1)} %v_hbm.1), custom_call_target="tpu_custom_call" | custom-call | tf_op jit(solution)/shard_map/pallas_call | solution.py:405
  30.9 1.0 %copy.7 = bf16[512,1024]{1,0:T(8,128)(2,1)} copy(bf16[512,1024]{1,0:T(8,128)(2,1)S(1)} %shard_map.55) | data formatting | bytes 2097152
